TPU v7x, 8 devices: a whole 2x2x1 slice. The times are simulated.
8 devices in a mesh: dp: 8 (over z, y, x, core).
Axes of the slice: x: 2, y: 2, z: 1, core: 2. Of those that a mesh axis runs over, the one named last changes fastest.
Arguments:
- hidden: bfloat16 [32768, 4096], P('dp')
- router_w: bfloat16 [4096, 128], replicated
- expert_idx: int32 [32768, 8], P('dp')
- gate_grad: float32 [32768, 8], P('dp')
Outputs:
- output 1: float32 [32768, 8], P('dp')
- output 2: float32 [], replicated
- output 3: bfloat16 [32768, 4096], P('dp')
- output 4: float32 [4096, 128], replicated
All inputs are finite; a program needn't handle non-finite values.
Results may differ from a plain program's by a relative error of at most 0.00790332.
Values sent between devices are 32-bit elements.
A program may use at most 1 GiB of HBM per device.

v0:
```python
import jax
import jax.numpy as jnp
from jax import lax
from jax.sharding import PartitionSpec as P

LOSS_ALPHA = 0.001


def gate_forward(hidden, router_w, expert_idx):
    logits = jnp.dot(hidden, router_w, preferred_element_type=jnp.float32)
    router_probs = jax.nn.softmax(logits, axis=-1)
    expert_ids = jnp.arange(router_w.shape[1], dtype=jnp.int32)
    idx_hits = expert_idx[:, :, None] == expert_ids[None, None, :]
    picked = jnp.sum(jnp.where(idx_hits, router_probs[:, None, :], 0.0), axis=2)
    pick_sum = jnp.sum(picked, axis=1, keepdims=True)
    return router_probs, idx_hits, pick_sum, picked / pick_sum


def logit_backward(router_probs, idx_hits, pick_sum, gate_probs, gate_grad, expert_freq, loss_scale, total_rows):
    num_experts = router_probs.shape[1]
    scaled_grad = loss_scale * gate_grad
    pick_grad = (scaled_grad - jnp.sum(scaled_grad * gate_probs, axis=1, keepdims=True)) / pick_sum
    aux_coef = loss_scale * LOSS_ALPHA * num_experts / total_rows
    prob_grad = jnp.sum(jnp.where(idx_hits, pick_grad[:, :, None], 0.0), axis=1) + aux_coef * expert_freq[None, :]
    logit_grad = router_probs * (prob_grad - jnp.sum(router_probs * prob_grad, axis=1, keepdims=True))
    return logit_grad.astype(jnp.bfloat16)


def solution(mesh):
    group_size = mesh.shape["dp"]

    def device_step(hidden, router_w, expert_idx, gate_grad):
        total_rows = hidden.shape[0] * group_size
        num_experts = router_w.shape[1]
        loss_scale = float(total_rows * num_experts * num_experts)
        router_probs, idx_hits, pick_sum, gate_probs = gate_forward(hidden, router_w, expert_idx)
        local_counts = jnp.sum(idx_hits, axis=(0, 1), dtype=jnp.float32)
        expert_freq = lax.psum(local_counts, "dp") / total_rows
        prob_mean = lax.psum(jnp.sum(router_probs, axis=0), "dp") / total_rows
        aux_loss = LOSS_ALPHA * num_experts * jnp.sum(expert_freq * prob_mean)
        grad_bf = logit_backward(router_probs, idx_hits, pick_sum, gate_probs, gate_grad, expert_freq, loss_scale, total_rows)
        hidden_grad = lax.dot_general(grad_bf, router_w, (((1,), (1,)), ((), ())), preferred_element_type=jnp.float32).astype(jnp.bfloat16)
        router_part = lax.dot_general(hidden, grad_bf, (((0,), (0,)), ((), ())), preferred_element_type=jnp.float32)
        router_grad = lax.psum(router_part, "dp")
        return gate_probs, aux_loss, hidden_grad, router_grad

    return jax.shard_map(device_step, mesh=mesh, in_specs=(P("dp", None), P(None, None), P("dp", None), P("dp", None)), out_specs=(P("dp", None), P(), P("dp", None), P(None, None)), check_vma=False)
```

profile of v0, /device:TPU:0, one launch (start us, length us, event | category | flops | bytes accessed | tf_op | source)
XLA Modules:
  0.0 236.1 jit_solution(18013661606128895021)
XLA Ops:
  7.2 0.0 copy-start
  7.2 0.0 all-reduce.2.cloned.1.call-start
  7.2 2.9 %copy.22 = s32[4096,8]{1,0:T(8,128)} copy(s32[4096,8]{0,1:T(8,128)} %param.6) | data formatting | bytes 262144 | tf_op args[2]
  10.2 0.0 copy-done
  10.2 15.3 %fusion.2 = (f32[4096]{0:T(1024)S(1)}, f32[4096,128]{0,1:T(8,128)S(1)}) fusion(bf16[4096,4096]{1,0:T(8,128)(2,1)} %param.4, bf16[4096,128]{1,0:T(8,128)(2,1)S(1)} %copy-done), kind=kOutput, calls=%fused_computation.17 | convolution fusion | flops 4295487488 | bytes 36716544 | tf_op jit(solution)/shard_map/dot_general | solution.py:10
  25.5 0.3 fusion.1
  25.8 1.6 fusion
  27.4 2.9 %copy.23 = f32[4096,128]{1,0:T(8,128)} copy(f32[4096,128]{0,1:T(8,128)} %fusion) | data formatting | bytes 4194304 | tf_op jit(solution)/shard_map/div | solution.py:11
  30.3 66.5 %select_reduce_fusion = (f32[4096]{0:T(1024)S(1)}, f32[4096,8]{1,0:T(8,128)}) fusion(f32[4096,128]{1,0:T(8,128)} %copy.23, s32[4096,8]{1,0:T(8,128)} %copy.22), kind=kLoop, calls=%fused_computation.1 | loop fusion | flops 16740352 | bytes 2375680 | tf_op jit(solution)/shard_map/reduce_sum | solution.py:15
  96.8 0.0 copy-start.4
  96.8 2.2 copy.24
  99.0 0.0 copy-done.4
  99.0 0.7 multiply_reduce_fusion.1
  99.7 1.9 copy.25
  101.6 25.7 %select_reduce_fusion.2 = (f32[4096,128]{1,0:T(8,128)}, f32[128]{0:T(128)S(1)}) fusion(f32[4096,8]{1,0:T(8,128)} %copy.25, s32[4096,8]{1,0:T(8,128)} %copy.22), kind=kLoop, calls=%fused_computation.3 | loop fusion | flops 24641408 | bytes 2359808 | tf_op jit(solution)/shard_map/reduce_sum | solution.py:24
  127.3 2.9 %copy.26 = f32[4096,128]{0,1:T(8,128)} copy(f32[4096,128]{1,0:T(8,128)} %get-tuple-element.20) | data formatting | bytes 4194304 | tf_op jit(solution)/shard_map/reduce_sum | solution.py:24
  130.2 25.2 %psum.21 = f32[128]{0:T(128)S(1)} all-reduce(f32[128]{0:T(128)S(1)} %get-tuple-element.21), channel_id=1, replica_groups=mesh['dp'=8] {'dp'}, use_global_device_ids=true, to_apply=%region_5.6 | all-reduce | flops 128 | bytes 1024 | tf_op jit(solution)/shard_map/psum | solution.py:38
  155.4 0.0 copy-start.1
  155.4 2.5 %multiply_reduce_fusion = (f32[4096]{0:T(1024)S(1)}, f32[128]{0:T(128)S(1)}) fusion(f32[4096,128]{0,1:T(8,128)} %copy.26, f32[128]{0:T(128)S(1)} %broadcast_multiply_fusion, f32[4096]{0:T(1024)S(1)} %fusion.1, f32[4096,128]{0,1:T(8,128)S(1)} %get-tuple-element.25, f32[4096]{0:T(1024)S(1)} %get-tuple-element.24), kind=kLoop, calls=%fused_computation.8 | loop fusion | flops 3141504 | bytes 4244480 | tf_op jit(solution)/shard_map/reduce_sum | solution.py:25
  157.9 0.0 copy-done.1
  157.9 0.6 multiply_convert_fusion
  158.5 0.0 copy-start.2
  158.5 1.0 copy-done.2
  159.4 14.3 %convolution_bitcast_fusion = f32[4096,128]{0,1:T(8,128)} fusion(bf16[4096,128]{0,1:T(8,128)(2,1)S(1)} %multiply_convert_fusion, bf16[4096,4096]{1,0:T(8,128)(2,1)} %param.4), kind=kOutput, calls=%fused_computation.6 | convolution fusion | flops 4294967296 | bytes 36700160 | tf_op jit(solution)/shard_map/dot_general | solution.py:43
  173.7 0.0 copy-start.3
  173.7 0.0 all-reduce.2.cloned.1.call-update
  173.7 23.4 %psum.22 = f32[128]{0:T(128)S(1)} all-reduce(f32[128]{0:T(128)S(1)} %get-tuple-element.19), channel_id=1, replica_groups=mesh['dp'=8] {'dp'}, use_global_device_ids=true, to_apply=%region_7.8 | all-reduce | flops 128 | bytes 1024 | tf_op jit(solution)/shard_map/psum | solution.py:39
  197.1 0.6 multiply_reduce_fusion.2
  198.4 0.0 copy-done.3
  198.4 14.3 %convolution_convert_fusion = bf16[4096,4096]{1,0:T(8,128)(2,1)} fusion(bf16[4096,128]{0,1:T(8,128)(2,1)S(1)} %copy-done.3, bf16[4096,128]{1,0:T(8,128)(2,1)S(1)} %copy-done), kind=kOutput, calls=%fused_computation | convolution fusion | flops 4311744512 | bytes 35651584 | tf_op jit(solution)/shard_map/dot_general | solution.py:42
  212.7 12.6 %all-reduce.2.cloned.1.call-done = f32[4096,128]{0,1:T(8,128)} async-done(((f32[4096,128]{0,1:T(8,128)}), f32[4096,128]{0,1:T(8,128)}) %all-reduce.2.cloned.1.call-update) | async-done | bytes 2097168 | tf_op jit(solution)/shard_map/psum | solution.py:44
  225.3 2.9 %copy.27 = f32[4096,128]{1,0:T(8,128)} copy(f32[4096,128]{0,1:T(8,128)} %all-reduce.2.cloned.1.call-done) | data formatting | bytes 4194304
  (2 shorter events, 0.0 us)
Async XLA Ops:
  7.2 3.0 %copy-start = (bf16[4096,128]{1,0:T(8,128)(2,1)S(1)}, bf16[4096,128]{1,0:T(8,128)(2,1)}, u32[]{:S(2)}) copy-start(bf16[4096,128]{1,0:T(8,128)(2,1)} %param.5) | copy-start | bytes 3145732
  7.2 218.1 %all-reduce.2.cloned.1.call-start = ((), (), s32[]{:S(2)}) async-start(), calls=%async_computation | async-start | bytes 4194304 | tf_op jit(solution)/shard_map/psum | solution.py:44
  96.8 2.2 copy-start.4
  155.4 2.5 %copy-start.1 = (f32[4096,128]{0,1:T(8,128)S(1)}, f32[4096,128]{0,1:T(8,128)}, u32[]{:S(2)}) copy-start(f32[4096,128]{0,1:T(8,128)} %copy.26) | copy-start | bytes 6291460
  158.5 1.0 copy-start.2
  173.7 24.7 %copy-start.3 = (bf16[4096,128]{0,1:T(8,128)(2,1)S(1)}, bf16[4096,128]{0,1:T(8,128)(2,1)}, u32[]{:S(2)}) copy-start(bf16[4096,128]{0,1:T(8,128)(2,1)} %copy-done.2) | copy-start | bytes 3145732
Sparse Core Ops, SparseCore 0:
  173.9 51.3 all-reduce.1
where the time goes:
time: 237 us; the launch traced here: 236 us
  other arithmetic  98.5 us (42%)
  blocking collectives  48.6 us (21%)
  matrix products  43.9 us (19%)
  local copies, waits for them, and re-layouts  16.7 us (7%)
  between operations  15.9 us (7%)
  waiting for transfers between devices  12.6 us (5%)
    reduce_sum x1, other arithmetic, gate_forward(): pick_sum = jnp.sum(picked, axis=1, keepdims=True)  66.5 us
    reduce_sum x1, other arithmetic, logit_backward(): jnp.sum(jnp.where(idx_hits, pick_grad[:, :, None], 0.0), axis=1)  25.7 us
    psum x1, blocking collectives, device_step(): expert_freq = lax.psum(local_counts, 'dp') / total_rows  25.2 us
    psum x1, blocking collectives, device_step(): prob_mean = lax.psum(jnp.sum(router_probs, axis=0), 'dp') / total_rows  23.4 us
    dot_general x1, matrix products, gate_forward(): logits = jnp.dot(hidden, router_w, preferred_element_type=jnp.float32)  15.3 us
    dot_general x1, matrix products, device_step(): lax.dot_general(grad_bf, router_w, (((1,), (1,)), ((), ())), preferred_el...  14.3 us
    dot_general x1, matrix products, device_step(): lax.dot_general(hidden, grad_bf, (((0,), (0,)), ((), ())), preferred_elem...  14.3 us
    psum x1, waiting for transfers between devices, device_step(): router_grad = lax.psum(router_part, 'dp')  12.6 us
  transfers between devices with their start and end apart: 1, of which 1 were waited for; matrix products, arithmetic and copies ran while one was open for 6% of the time, Pallas kernels for 0%

commit v1 on v0

v1 whole, which is shorter than its diff:
```python
import jax
import jax.numpy as jnp
from jax import lax
from jax.experimental import pallas as pl
from jax.experimental.pallas import tpu as pltpu
from jax.sharding import PartitionSpec as P

LOSS_ALPHA = 0.001
MESH = pl.DeviceIdType.MESH
LANES = 128


def neighbours():
    me = lax.axis_index("dp")
    core, x, y = me % 2, (me // 2) % 2, me // 4
    def at(flip):
        fy, fx, fc = (flip // 4) % 2, (flip // 2) % 2, flip % 2
        return (1 - y if fy else y) * 4 + (1 - x if fx else x) * 2 + (1 - core if fc else core)
    return me, at


def remote(src, dst, send_sem, recv_sem, device):
    return pltpu.make_async_remote_copy(src_ref=src, dst_ref=dst, send_sem=send_sem, recv_sem=recv_sem, device_id=(device,), device_id_type=MESH)


def router_kernel(total_rows, hidden_hbm, w_hbm, idx_hbm, gg_hbm, gate_ref, aux_ref, gt_ref, rg_hbm,
                  hid, w, idx, gg, logit_t, count_acc, prob_acc, f_bcast, cnt, prob, send_part, own, from_part, from_x, from_y, gather,
                  load_sem, small_sem, cnt_send, cnt_recv, prob_send, prob_recv, part_send, part_recv, x_send, x_recv, y_send, y_recv,
                  gat_send, gat_recv, out_sem):
    rows, width = hid.shape
    experts, top_k = w.shape[1], idx.shape[0]
    shard = width // 8
    half = experts // 2
    block = 256
    blocks = rows // block
    me, at = neighbours()
    core = me % 2
    chip = me // 2
    loss_scale = float(total_rows * experts * experts)
    aux_coef = loss_scale * LOSS_ALPHA * experts / total_rows

    small = [pltpu.make_async_copy(idx_hbm, idx, small_sem.at[0]), pltpu.make_async_copy(w_hbm, w, small_sem.at[1]), pltpu.make_async_copy(gg_hbm, gg, small_sem.at[2])]
    for c in small:
        c.start()

    def load(b):
        part = pl.ds(b * block, block)
        return pltpu.make_async_copy(hidden_hbm.at[part], hid.at[part], load_sem.at[b])

    for b in range(blocks):
        load(b).start()

    barrier = pltpu.get_barrier_semaphore()
    for k in range(1, 8):
        pl.semaphore_signal(barrier, inc=1, device_id=(at(k),), device_id_type=MESH)

    expert_id = lax.broadcasted_iota(jnp.int32, (experts, LANES), 0)

    def hits(t):
        ids = idx[:, pl.ds(t * LANES, LANES)]
        return [expert_id == ids[j:j + 1, :] for j in range(top_k)]

    def count_tile(t):
        total = count_acc[...]
        for hit in hits(t):
            total = total + jnp.where(hit, 1.0, 0.0)
        count_acc[...] = total

    def logits(b):
        load(b).wait()
        part = pl.ds(b * block, block)
        out = jnp.dot(hid[part, :], w[...], preferred_element_type=jnp.float32)
        logit_t[:, part] = out.T

    def backward_tile(t):
        part = pl.ds(t * LANES, LANES)
        hit = hits(t)
        val = logit_t[:, part]
        val = jnp.exp(val - jnp.max(val, axis=0, keepdims=True))
        p = val * (1.0 / jnp.sum(val, axis=0, keepdims=True))
        prob_acc[...] += p
        picked = jnp.concatenate([jnp.sum(jnp.where(h, p, 0.0), axis=0, keepdims=True) for h in hit], axis=0)
        pick_sum = jnp.sum(picked, axis=0, keepdims=True)
        gates = picked / pick_sum
        gate_ref[:, part] = gates
        scaled = loss_scale * gg[:, part]
        pick_grad = (scaled - jnp.sum(scaled * gates, axis=0, keepdims=True)) / pick_sum
        prob_grad = jnp.zeros_like(p)
        for j in range(top_k):
            prob_grad = jnp.where(hit[j], pick_grad[j:j + 1, :], prob_grad)
        prob_grad = prob_grad + f_bcast[...]
        grad = p * (prob_grad - jnp.sum(p * prob_grad, axis=0, keepdims=True))
        gt_ref[:, part] = grad.astype(jnp.bfloat16)

    small[0].wait()
    count_acc[...] = jnp.zeros_like(count_acc)
    prob_acc[...] = jnp.zeros_like(prob_acc)
    small[1].wait()
    tiles = rows // LANES
    first = 4

    @pl.loop(0, first)
    def _(b):
        logits(b)
        for u in range(tiles // first):
            count_tile(b * (tiles // first) + u)

    def exchange(buf, send, recv):
        return [remote(buf.at[me], buf.at[me], send.at[k], recv.at[k], at(k)) for k in range(1, 8)]

    cnt[me] = jnp.broadcast_to(jnp.sum(count_acc[...].T, axis=0, keepdims=True), (8, LANES))
    pl.semaphore_wait(barrier, 7)
    cnt_copies = exchange(cnt, cnt_send, cnt_recv)
    for c in cnt_copies:
        c.start()

    @pl.loop(first, blocks // 2)
    def _(b):
        logits(b)

    for c in cnt_copies:
        c.wait()
    freq = jnp.sum(cnt[...], axis=0) * (1.0 / total_rows)
    f_bcast[...] = jnp.broadcast_to(aux_coef * freq[:1, :], (experts, LANES)).T
    small[2].wait()

    @pl.loop(blocks // 2, blocks - 1)
    def _(b):
        logits(b)
        for u in range(4):
            backward_tile((b - blocks // 2) * 4 + u)

    logits(blocks - 1)
    for u in range(4):
        backward_tile(tiles - 4 + u)

    prob[me] = jnp.broadcast_to(jnp.sum(prob_acc[...].T, axis=0, keepdims=True), (8, LANES))
    prob_copies = exchange(prob, prob_send, prob_recv)

    def chip_at(flip):
        return at(2 * flip) // 2

    def columns(s):
        return pl.ds(pl.multiple_of(s * shard, shard), shard)

    def part_copy(i):
        return remote(send_part.at[i], from_part.at[i], part_send.at[i], part_recv.at[i], at(1))

    low, high = pl.ds(0, half), pl.ds(half, half)

    def x_copy(i, src):
        return remote(src, from_x.at[i], x_send.at[i], x_recv.at[i], at(2))

    def y_copy(i, src):
        return remote(src, from_y.at[i], y_send.at[i], y_recv.at[i], at(4))

    def combine(i):
        part_copy(i).wait_recv()
        own[i] = own[i] + from_part[i]

    y, x = chip // 2, chip % 2

    @pl.loop(0, 4)
    def _(i):
        flip = 3 - i
        fy, fx = flip // 2, flip % 2
        target = (y + fy) % 2 * 2 + (x + fx) % 2
        send_part[i] = jnp.dot(gt_ref[...], hid[:, columns(target * 2 + (1 - core))], preferred_element_type=jnp.float32)
        part_copy(i).start()

        @pl.when(i == 1)
        def _():
            combine(0)
            x_copy(0, own.at[0, low]).start()
            y_copy(0, own.at[0, high]).start()

        @pl.when(i == 2)
        def _():
            combine(1)
            y_copy(1, own.at[1, high]).start()

        @pl.when(i == 3)
        def _():
            combine(2)
            x_copy(1, own.at[2, low]).start()

        own[i] = jnp.dot(gt_ref[...], hid[:, columns(target * 2 + core)], preferred_element_type=jnp.float32)

    for c in prob_copies:
        c.start()

    x_copy(0, own.at[0, low]).wait_recv()
    own[1, low] = own[1, low] + from_x[0]
    y_copy(2, own.at[1, low]).start()
    y_copy(0, own.at[0, high]).wait_recv()
    own[2, high] = own[2, high] + from_y[0]
    x_copy(2, own.at[2, high]).start()

    combine(3)
    x_copy(1, own.at[2, low]).wait_recv()
    own[3, low] = own[3, low] + from_x[1]
    y_copy(1, own.at[1, high]).wait_recv()
    own[3, high] = own[3, high] + from_y[1]

    for c in prob_copies:
        c.wait()
    prob_mean = jnp.sum(prob[...], axis=0) * (1.0 / total_rows)
    freq_again = jnp.sum(cnt[...], axis=0) * (1.0 / total_rows)
    aux_ref[...] = jnp.broadcast_to(LOSS_ALPHA * experts * jnp.sum(freq_again * prob_mean, axis=1, keepdims=True), (8, LANES))

    y_copy(2, own.at[1, low]).wait_recv()
    own[3, low] = own[3, low] + from_y[2]
    x_copy(2, own.at[2, high]).wait_recv()
    own[3, high] = own[3, high] + from_x[2]
    gather[me] = own[3].T

    mine, xs, ys, ds = me, at(2), at(4), at(6)
    top, bottom = pl.ds(0, shard // 2), pl.ds(shard // 2, shard // 2)

    def gat_copy(k, src, device):
        return remote(src, src, gat_send.at[k], gat_recv.at[k], device)

    def out_copy(k, s):
        return pltpu.make_async_copy(gather.at[s], rg_hbm.at[pl.ds(pl.multiple_of(s * shard, shard), shard)], out_sem.at[k])

    to_x = gat_copy(0, gather.at[mine], at(2))
    to_y = gat_copy(1, gather.at[mine], at(4))
    to_p = gat_copy(4, gather.at[mine], at(1))
    to_x.start()
    to_y.start()
    to_p.start()
    out_copy(0, mine).start()
    to_x.wait_recv()
    fwd_y = gat_copy(2, gather.at[xs, top], at(4))
    fwd_y.start()
    part_x = gat_copy(5, gather.at[xs], at(1))
    part_x.start()
    out_copy(1, xs).start()
    to_y.wait_recv()
    fwd_x = gat_copy(3, gather.at[ys, bottom], at(2))
    fwd_x.start()
    part_y = gat_copy(6, gather.at[ys], at(1))
    part_y.start()
    out_copy(2, ys).start()
    fwd_y.wait_recv()
    fwd_x.wait_recv()
    part_d = gat_copy(7, gather.at[ds], at(1))
    part_d.start()
    out_copy(3, ds).start()
    to_p.wait_recv()
    out_copy(4, at(1)).start()
    part_x.wait_recv()
    out_copy(5, at(3)).start()
    part_y.wait_recv()
    out_copy(6, at(5)).start()
    part_d.wait_recv()
    out_copy(7, at(7)).start()

    @pl.loop(0, 4)
    def _(i):
        part_copy(i).wait_send()

    for i, src in enumerate((own.at[0, low], own.at[2, low], own.at[2, high])):
        x_copy(i, src).wait_send()
    for i, src in enumerate((own.at[0, high], own.at[1, high], own.at[1, low])):
        y_copy(i, src).wait_send()
    for c in (to_x, to_y, fwd_y, fwd_x, to_p, part_x, part_y, part_d):
        c.wait_send()
    for k, s in enumerate((mine, xs, ys, ds, at(1), at(3), at(5), at(7))):
        out_copy(k, s).wait()


def grad_kernel(gt_ref, w_ref, gate_in, aux_in, rg_in, hg_ref, gate_ref, aux_ref, rg_ref):
    out = lax.dot_general(gt_ref[...], w_ref[...], (((0,), (1,)), ((), ())), preferred_element_type=jnp.float32)
    hg_ref[...] = out.astype(jnp.bfloat16)
    gate_ref[...] = gate_in[...]
    aux_ref[...] = aux_in[...]
    rg_ref[...] = rg_in[...]


def solution(mesh):
    group_size = mesh.shape["dp"]

    def device_step(hidden, router_w, expert_idx, gate_grad):
        rows, width = hidden.shape
        experts, top_k = router_w.shape[1], expert_idx.shape[1]
        shard = width // 8
        f32, bf16 = jnp.float32, jnp.bfloat16
        any_spec, vmem_spec = pl.BlockSpec(memory_space=pl.ANY), pl.BlockSpec(memory_space=pltpu.VMEM)
        dma, vmem = pltpu.SemaphoreType.DMA, pltpu.VMEM

        def body(*refs):
            router_kernel(rows * group_size, *refs)

        gates, aux, gt, rg = pl.pallas_call(
            body,
            out_shape=(jax.ShapeDtypeStruct((top_k, rows), f32), jax.ShapeDtypeStruct((8, LANES), f32), jax.ShapeDtypeStruct((experts, rows), bf16), jax.ShapeDtypeStruct((width, experts), f32)),
            in_specs=[any_spec] * 4,
            out_specs=(vmem_spec, vmem_spec, vmem_spec, any_spec),
            scratch_shapes=[
                vmem((rows, width), bf16), vmem((width, experts), bf16), vmem((top_k, rows), jnp.int32), vmem((top_k, rows), f32),
                vmem((experts, rows), f32), vmem((experts, LANES), f32), vmem((experts, LANES), f32), vmem((experts, LANES), f32),
                vmem((8, 8, LANES), f32), vmem((8, 8, LANES), f32),
                vmem((4, experts, shard), f32), vmem((4, experts, shard), f32), vmem((4, experts, shard), f32),
                vmem((3, experts // 2, shard), f32), vmem((3, experts // 2, shard), f32), vmem((8, shard, experts), f32),
                dma((rows // 256,)), dma((3,)), dma((8,)), dma((8,)), dma((8,)), dma((8,)), dma((4,)), dma((4,)),
                dma((3,)), dma((3,)), dma((3,)), dma((3,)), dma((8,)), dma((8,)), dma((8,)),
            ],
            compiler_params=pltpu.CompilerParams(collective_id=0, has_side_effects=True, vmem_limit_bytes=56 * 2**20),
            name="router",
        )(hidden, router_w, expert_idx.T, gate_grad.T)

        steps = 16
        block, part = rows // steps, width // steps
        hidden_grad, gates, aux, rg = pl.pallas_call(
            grad_kernel,
            grid=(steps,),
            out_shape=(jax.ShapeDtypeStruct((rows, width), bf16), jax.ShapeDtypeStruct((top_k, rows), f32), jax.ShapeDtypeStruct((8, LANES), f32), jax.ShapeDtypeStruct((width, experts), f32)),
            in_specs=[
                pl.BlockSpec((experts, block), lambda i: (0, i)), pl.BlockSpec((width, experts), lambda i: (0, 0)), pl.BlockSpec((top_k, block), lambda i: (0, i)),
                pl.BlockSpec((8, LANES), lambda i: (0, 0)), pl.BlockSpec((part, experts), lambda i: (i, 0)),
            ],
            out_specs=(pl.BlockSpec((block, width), lambda i: (i, 0)), pl.BlockSpec((top_k, block), lambda i: (0, i)), pl.BlockSpec((8, LANES), lambda i: (0, 0)), pl.BlockSpec((part, experts), lambda i: (i, 0))),
            compiler_params=pltpu.CompilerParams(vmem_limit_bytes=40 * 2**20),
            name="hidden_grad",
        )(gt, router_w, gates, aux, rg)
        return gates.T, aux[0, 0], hidden_grad, rg

    return jax.shard_map(device_step, mesh=mesh, in_specs=(P("dp", None), P(None, None), P("dp", None), P("dp", None)), out_specs=(P("dp", None), P(), P("dp", None), P(None, None)), check_vma=False)
```

time: 237 us -> 84.4 us (0.36)
  other arithmetic: 98.5 us -> 0 us
  Pallas kernels: 0 us -> 78.4 us
  blocking collectives: 48.6 us -> 0 us
  matrix products: 43.9 us -> 0 us
  between operations: 15.9 us -> 0.67 us
  waiting for transfers between devices: 12.6 us -> 0 us
  local copies, waits for them, and re-layouts: 16.7 us -> 4.91 us
    reduce_sum x6 -> x0, other arithmetic: 96.3 us -> none  [the longest x1 66.5 us: gate_forward(): pick_sum = jnp.sum(picked, axis=1, keepdims=True)]
    pallas_call x0 -> x2, Pallas kernels: none -> 78.4 us  [the longest x1 61.2 us: device_step(): pl.pallas_call(body, out_shape=(jax.ShapeDtypeStruct((top_k, rows), f32),...]
    psum x2 -> x0, blocking collectives: 48.6 us -> none  [the longest x1 25.2 us: device_step(): expert_freq = lax.psum(local_counts, 'dp') / total_rows]
    dot_general x3 -> x0, matrix products: 43.9 us -> none  [the longest x1 15.3 us: gate_forward(): logits = jnp.dot(hidden, router_w, preferred_element_type=jnp.float32)]
    psum x1 -> x0, waiting for transfers between devices: 12.6 us -> none  [device_step(): router_grad = lax.psum(router_part, 'dp')]
    reduce_sum x2 -> x0, local copies, waits for them, and re-layouts: 5.07 us -> none  [the longest x1 2.88 us: logit_backward(): jnp.sum(jnp.where(idx_hits, pick_grad[:, :, None], 0.0), axis=1)]
    div x2 -> x0, local copies, waits for them, and re-layouts: 4.81 us -> none  [the longest x1 2.88 us: gate_forward(): router_probs = jax.nn.softmax(logits, axis=-1)]
    unnamed x12 -> x10, local copies, waits for them, and re-layouts: 6.81 us -> 4.4 us
  transfers between devices with their start and end apart: 1 -> 0, of which waited for: 1 -> 0; matrix products, arithmetic and copies ran while one was open for 6% -> 0% of each run, Pallas kernels for 0% -> 0%
where the time goes in v1:
time: 84.4 us; the launch traced here: 84 us
  Pallas kernels  78.4 us (93%)
  local copies, waits for them, and re-layouts  4.91 us (6%)
    pallas_call x1, Pallas kernels, device_step(): pl.pallas_call(body, out_shape=(jax.ShapeDtypeStruct((top_k, rows), f32),...  61.2 us
    pallas_call x1, Pallas kernels, device_step(): pl.pallas_call(grad_kernel, grid=(steps,), out_shape=(jax.ShapeDtypeStruc...  17.2 us
    unnamed x10, local copies, waits for them, and re-layouts  4.4 us

profile of v1, /device:TPU:0, one launch (start us, length us, event | category | flops | bytes accessed | tf_op | source)
XLA Modules:
  0.0 84.0 jit_solution(11789065402744080377)
XLA Ops:
  0.6 0.0 copy-start
  0.6 61.2 %router.1 = (f32[8,4096]{1,0:T(8,128)}, f32[8,128]{1,0:T(8,128)}, bf16[128,4096]{1,0:T(8,128)(2,1)}, f32[4096,128]{1,0:T(8,128)}) custom-call(bf16[4096,4096]{1,0:T(8,128)(2,1)} %refs_0_.1, bf16[4096,128]{1,0:T(8,128)(2,1)} %w_ref.1, s32[8,4096]{1,0:T(8,128)} %bitcast.4, f32[8,4096]{1,0:T(8,128)} %bitcast.5), custom_call_target="tpu_custom_call" | custom-call | tf_op jit(solution)/shard_map/router/pallas_call | solution.py:295
  61.8 0.0 copy-done
  61.9 0.0 copy-start.1
  61.9 1.6 %copy-done.1 = f32[4096,128]{1,0:T(8,128)S(1)} copy-done((f32[4096,128]{1,0:T(8,128)S(1)}, f32[4096,128]{1,0:T(8,128)}, u32[]{:S(2)}) %copy-start.1) | copy-done | bytes 2097176
  63.4 0.0 copy-start.2
  63.4 1.2 %copy-done.2 = bf16[128,4096]{1,0:T(8,128)(2,1)S(1)} copy-done((bf16[128,4096]{1,0:T(8,128)(2,1)S(1)}, bf16[128,4096]{1,0:T(8,128)(2,1)}, u32[]{:S(2)}) %copy-start.2) | copy-done | bytes 1048600
  64.7 0.0 copy-start.3
  64.7 0.9 %copy-done.3 = f32[8,4096]{1,0:T(8,128)S(1)} copy-done((f32[8,4096]{1,0:T(8,128)S(1)}, f32[8,4096]{1,0:T(8,128)}, u32[]{:S(2)}) %copy-start.3) | copy-done | bytes 131096
  65.6 0.0 copy-start.4
  65.6 0.7 copy-done.4
  66.3 17.2 %hidden_grad.1 = (bf16[4096,4096]{1,0:T(8,128)(2,1)}, f32[8,4096]{1,0:T(8,128)}, f32[8,128]{1,0:T(8,128)S(1)}, f32[4096,128]{1,0:T(8,128)}) custom-call(bf16[128,4096]{1,0:T(8,128)(2,1)S(1)} %copy-done.2, bf16[4096,128]{1,0:T(8,128)(2,1)S(1)} %copy-done, f32[8,4096]{1,0:T(8,128)S(1)} %copy-done.3, f32[8,128]{1,0:T(8,128)S(1)} %copy-done.4, ...), custom_call_target="tpu_custom_call" | custom-call | tf_op jit(solution)/shard_map/hidden_grad/pallas_call | solution.py:315
  83.5 0.5 slice.3
Async XLA Ops:
  0.6 61.2 %copy-start = (bf16[4096,128]{1,0:T(8,128)(2,1)S(1)}, bf16[4096,128]{1,0:T(8,128)(2,1)}, u32[]{:S(2)}) copy-start(bf16[4096,128]{1,0:T(8,128)(2,1)} %w_ref.1) | copy-start | bytes 3145732
  61.9 1.6 %copy-start.1 = (f32[4096,128]{1,0:T(8,128)S(1)}, f32[4096,128]{1,0:T(8,128)}, u32[]{:S(2)}) copy-start(f32[4096,128]{1,0:T(8,128)} %get-tuple-element.15.rg_in) | copy-start | bytes 6291460
  63.4 1.2 %copy-start.2 = (bf16[128,4096]{1,0:T(8,128)(2,1)S(1)}, bf16[128,4096]{1,0:T(8,128)(2,1)}, u32[]{:S(2)}) copy-start(bf16[128,4096]{1,0:T(8,128)(2,1)} %get-tuple-element.12.gt_ref) | copy-start | bytes 3145732
  64.7 0.9 %copy-start.3 = (f32[8,4096]{1,0:T(8,128)S(1)}, f32[8,4096]{1,0:T(8,128)}, u32[]{:S(2)}) copy-start(f32[8,4096]{1,0:T(8,128)} %get-tuple-element.13.gate_in) | copy-start | bytes 393220
  65.6 0.7 copy-start.4
